TPU v7x, 32 devices: a whole 2x2x4 slice. The times are simulated.
32 devices in a mesh: groups: 2 (over x), ep: 8 (over z, y), tp: 2 (over core).
Axes of the slice: x: 2, y: 2, z: 4, core: 2. Of those that a mesh axis runs over, the one named last changes fastest.
Arguments:
- hidden: bfloat16 [256, 3584], P(('groups', 'ep'), 'tp'), parts along dimension 0, may hold values from -6 to 6
- routes: int32 [256, 4], P(('groups', 'ep')), parts along dimension 0, may hold values from 0 to 7, as said below
- router_weight: bfloat16 [3584, 8], P('tp'), may hold values from -0.1875 to 0.1875
- gate_weight: bfloat16 [8, 3584, 1024], P('ep', None, 'tp'), may hold values from -0.09375 to 0.09375
- up_weight: bfloat16 [8, 3584, 1024], P('ep', None, 'tp'), may hold values from -0.09375 to 0.09375
- down_weight: bfloat16 [8, 1024, 3584], P('ep', 'tp'), may hold values from -0.1875 to 0.1875
- q_latent: bfloat16 [64, 64, 512], P(('groups', 'ep'), 'tp'), parts along dimension 0, may hold values from -48 to 48
- q_rope: bfloat16 [64, 64, 64], P(('groups', 'ep'), 'tp'), parts along dimension 0, may hold values from -48 to 48
- cache_latent: bfloat16 [64, 256, 512], P(('groups', 'ep')), parts along dimension 0, may hold values from -4 to 4
- cache_rope: bfloat16 [64, 64, 256], P(('groups', 'ep')), parts along dimension 0, may hold values from -4 to 4
- lengths: int32 [64], P(('groups', 'ep')), parts along dimension 0, may hold values from 16 to 256, as said below
Outputs:
- moe_out: bfloat16 [256, 3584], P(('groups', 'ep'), 'tp'), parts along dimension 0
- attn_latent: bfloat16 [64, 64, 512], P(('groups', 'ep'), 'tp'), parts along dimension 0
There are 2 independent parts, one for each index of `groups`. A program takes and returns all parts, laid end to end along the dimension named above; an argument that names none is the same for every part. Nothing has to cross between parts.
Inputs may be any that keep to these rules, and one draw needn't show every extreme that they name: `routes`: each row names 4 different experts; in each aligned block of 16 rows (the rows of one index of ep) no expert is named more than 16 times, and one expert, the same in every block, is named exactly 16 times in each block. `lengths`: one sequence has 256 live positions and one has 16.
All inputs are finite; a program needn't handle non-finite values.
Results may differ from a plain program's by a relative error of at most 0.0085.
Values may be sent and summed in bfloat16 or wider, within the bound.
A program may use at most 128 MiB of HBM per device.

v0:
```python
import jax
import jax.numpy as jnp
from jax import lax
from jax.sharding import PartitionSpec as P

softmax_scale = 192.0 ** (-0.5)
routed_scale = 2.5


def local(
    hidden,
    routes,
    router_weight,
    gate_weight,
    up_weight,
    down_weight,
    q_latent,
    q_rope,
    cache_latent,
    cache_rope,
    lengths,
):
    token_count, top_count = routes.shape
    expert_count = lax.axis_size("ep")
    capacity = min(token_count, 4 * token_count * top_count // expert_count)
    partial_logits = jnp.dot(hidden, router_weight, preferred_element_type=jnp.float32)
    logits = lax.psum(partial_logits, "tp")
    affinity = jax.nn.sigmoid(logits)
    expert_iota = jnp.arange(expert_count, dtype=jnp.int32)
    chosen_mask = routes[:, :, None] == expert_iota[None, None, :]
    chosen = jnp.sum(jnp.where(chosen_mask, affinity[:, None, :], 0.0), axis=2)
    gates = routed_scale * chosen / jnp.sum(chosen, axis=1, keepdims=True)
    flat_mask = chosen_mask.reshape(token_count * top_count, expert_count).astype(jnp.int32)
    earlier = jnp.cumsum(flat_mask, axis=0) - flat_mask
    within = jnp.sum(flat_mask * earlier, axis=1).reshape(token_count, top_count)
    slot_index = routes * capacity + within
    slot_iota = jnp.arange(expert_count * capacity, dtype=jnp.int32)
    placing = jnp.sum(
        (slot_index[None, :, :] == slot_iota[:, None, None]).astype(jnp.int32), axis=2
    )
    placing = placing.astype(jnp.bfloat16)
    outgoing = jnp.dot(placing, hidden, preferred_element_type=jnp.float32).astype(jnp.bfloat16)
    outgoing = outgoing.reshape(expert_count, capacity, hidden.shape[1])
    received = lax.all_to_all(outgoing, "ep", split_axis=0, concat_axis=0, tiled=True)
    received = lax.all_gather(received, "tp", axis=2, tiled=True)
    source_count, slot_count, feature_count = received.shape
    flat_rows = received.reshape(source_count * slot_count, feature_count)
    gate_part = jnp.dot(flat_rows, gate_weight[0], preferred_element_type=jnp.float32)
    up_part = jnp.dot(flat_rows, up_weight[0], preferred_element_type=jnp.float32)
    active = (jax.nn.silu(gate_part) * up_part).astype(jnp.bfloat16)
    partial_out = jnp.dot(active, down_weight[0], preferred_element_type=jnp.float32)
    summed = lax.psum_scatter(partial_out, "tp", scatter_dimension=1, tiled=True).astype(
        jnp.bfloat16
    )
    summed = summed.reshape(source_count, slot_count, summed.shape[1])
    returned = lax.all_to_all(summed, "ep", split_axis=0, concat_axis=0, tiled=True)
    scores = jnp.einsum("bhl,bjl->bhj", q_latent, cache_latent, preferred_element_type=jnp.float32)
    scores = scores + jnp.einsum(
        "bhr,brj->bhj", q_rope, cache_rope, preferred_element_type=jnp.float32
    )
    scores = scores * softmax_scale
    position = jnp.arange(cache_latent.shape[1], dtype=jnp.int32)
    live = position[None, None, :] < lengths[:, None, None]
    scores = jnp.where(live, scores, -jnp.inf)
    highest = jnp.max(scores, axis=2, keepdims=True)
    expo = jnp.where(live, jnp.exp(scores - highest), 0.0)
    attn_probs = (expo / jnp.sum(expo, axis=2, keepdims=True)).astype(jnp.bfloat16)
    attn_latent = jnp.einsum(
        "bhj,bjl->bhl", attn_probs, cache_latent, preferred_element_type=jnp.float32
    )
    attn_latent = attn_latent.astype(jnp.bfloat16)
    returned_flat = returned.reshape(expert_count * capacity, returned.shape[2])
    picked = jnp.take(returned_flat, slot_index.reshape(-1), axis=0).reshape(
        token_count, top_count, returned.shape[2]
    )
    moe_out = jnp.sum(gates[:, :, None] * picked.astype(jnp.float32), axis=1).astype(jnp.bfloat16)
    return (moe_out, attn_latent)


def solution(mesh):
    return jax.shard_map(
        local,
        mesh=mesh,
        in_specs=(
            P(("groups", "ep"), "tp"),
            P(("groups", "ep"), None),
            P("tp", None),
            P("ep", None, "tp"),
            P("ep", None, "tp"),
            P("ep", "tp", None),
            P(("groups", "ep"), "tp", None),
            P(("groups", "ep"), "tp", None),
            P(("groups", "ep"), None, None),
            P(("groups", "ep"), None, None),
            P(("groups", "ep")),
        ),
        out_specs=(P(("groups", "ep"), "tp"), P(("groups", "ep"), "tp", None)),
        check_vma=False,
    )
```

profile of v0, /device:TPU:0, one launch (start us, length us, event | category | flops | bytes accessed | tf_op | source)
XLA Modules:
  0.0 79.6 jit_solution(17327252212873637987)
XLA Ops:
  7.2 0.0 copy-start
  7.2 0.0 reduce-scatter.2.cloned.1.call-start
  7.2 0.8 %copy.22 = s32[16,4]{1,0:T(8,128)S(1)} copy(s32[16,4]{0,1:T(4,128)} %param.12) | data formatting | bytes 512 | tf_op args[1]
  8.1 0.1 eq.38
  8.2 0.1 fusion.27
  8.2 0.1 reduce_window_sum.11
  8.3 0.2 select_reduce_fusion
  8.5 0.1 reshape.109
  8.6 0.1 copy.24
  8.7 0.1 convert_reduce_fusion
  8.8 1.1 %convolution_convert_fusion = bf16[128,1792]{1,0:T(8,128)(2,1)S(1)} fusion(bf16[16,1792]{1,0:T(8,128)(2,1)} %param.11, s32[128,16]{0,1:T(8,128)S(1)} %convert_reduce_fusion), kind=kOutput, calls=%fused_computation.8 | convolution fusion | flops 7571456 | bytes 524288 | tf_op jit(solution)/shard_map/dot_general | solution.py:42
  9.9 20.3 %all_to_all.10 = bf16[8,16,1792]{2,1,0:T(8,128)(2,1)S(1)} all-to-all(bf16[8,16,1792]{2,1,0:T(8,128)(2,1)S(1)} %bitcast.36), channel_id=1, replica_groups=mesh['groups'=2,'ep'=8,'tp'=2] {'ep'}, dimensions={0} | all-to-all | bytes 917504 | tf_op jit(solution)/shard_map/all_to_all | solution.py:44
  30.2 2.5 %all_gather.3 = bf16[8,16,3584]{2,1,0:T(8,128)(2,1)S(1)} all-gather(bf16[8,16,1792]{2,1,0:T(8,128)(2,1)S(1)} %all_to_all.10), channel_id=1, replica_groups=mesh['groups'=2,'ep'=8,'tp'=2] {'tp'}, dimensions={2}, use_global_device_ids=true | all-gather | bytes 1376256 | tf_op jit(solution)/shard_map/all_gather | solution.py:45
  32.7 2.7 %fusion.5 = f32[128,512]{1,0:T(8,128)S(1)} fusion(bf16[128,3584]{1,0:T(8,128)(2,1)S(1)} %bitcast.34, bf16[1,3584,512]{2,1,0:T(8,128)(2,1)} %param.14), kind=kOutput, calls=%fused_computation.6 | convolution fusion | flops 469762048 | bytes 4849664 | tf_op jit(solution)/shard_map/dot_general | solution.py:48
  35.4 5.7 %fusion.1 = f32[128,3584]{1,0:T(8,128)} fusion(bf16[1,512,3584]{2,1,0:T(8,128)(2,1)} %param.16, bf16[128,3584]{1,0:T(8,128)(2,1)S(1)} %bitcast.35, bf16[1,3584,512]{2,1,0:T(8,128)(2,1)} %param.15, f32[128,512]{1,0:T(8,128)S(1)} %fusion.5), kind=kOutput, calls=%fused_computation.2 | convolution fusion | flops 939917312 | bytes 10354688 | tf_op jit(solution)/shard_map/dot_general | solution.py:51
  41.1 0.0 reduce-scatter.2.cloned.1.call-update
  41.1 0.1 reshape.114
  41.2 0.1 fusion.34
  41.3 2.5 %psum.7 = f32[16,8]{0,1:T(8,128)S(1)} all-reduce(f32[16,8]{0,1:T(8,128)S(1)} %fusion.34), channel_id=1, replica_groups=mesh['groups'=2,'ep'=8,'tp'=2] {'tp'}, use_global_device_ids=true, to_apply=%region_0.0 | all-reduce | flops 128 | bytes 1024 | tf_op jit(solution)/shard_map/psum | solution.py:27
  43.9 0.1 copy.21
  44.0 0.4 fusion.35
  44.4 5.2 %reduce-scatter.2.cloned.1.call-done = f32[128,1792]{1,0:T(8,128)} async-done(((f32[128,3584]{1,0:T(8,128)}), f32[128,1792]{1,0:T(8,128)}) %reduce-scatter.2.cloned.1.call-update) | async-done | bytes 917520 | tf_op jit(solution)/shard_map/reduce_scatter | solution.py:52
  49.6 2.0 %convert_element_type.35 = bf16[128,1792]{1,0:T(8,128)(2,1)} convert(f32[128,1792]{1,0:T(8,128)} %reduce-scatter.2.cloned.1.call-done) | non-fusion elementwise | flops 229376 | bytes 1376256 | tf_op jit(solution)/shard_map/convert_element_type | solution.py:52
  51.6 5.9 %all-to-all-start.1 = ((bf16[8,16,1792]{2,1,0:T(8,128)(2,1)}), bf16[8,16,1792]{2,1,0:T(8,128)(2,1)S(1)}, u32[]{:S(2)}, u32[]{:S(2)}) async-start(bf16[8,16,1792]{2,1,0:T(8,128)(2,1)} %bitcast.5), calls=%async_computation.2 | async-start | bytes 917504 | tf_op jit(solution)/shard_map/all_to_all | solution.py:56
  57.4 0.1 iota_compare_fusion.3
  57.5 0.2 fusion.17
  57.7 0.2 fusion.33
  57.9 1.0 %convolution_convert_fusion.1 = bf16[4,32,512]{2,1,0:T(8,128)(2,1)} fusion(bf16[4,256,512]{2,1,0:T(8,128)(2,1)S(1)} %copy-done, f32[4,32]{1,0:T(4,128)S(1)} %fusion.33, f32[4,32,256]{2,1,0:T(8,128)S(1)} %fusion.17, pred[4,256]{1,0:T(4,128)(4,1)S(1)} %iota_compare_fusion.3), kind=kOutput, calls=%fused_computation.11 | convolution fusion | flops 33751424 | bytes 1312256 | tf_op jit(solution)/shard_map/bhj,bjl->bhl/dot_general | solution.py:68
  58.8 12.0 %all-to-all-done.1 = bf16[8,16,1792]{2,1,0:T(8,128)(2,1)S(1)} async-done(((bf16[8,16,1792]{2,1,0:T(8,128)(2,1)}), bf16[8,16,1792]{2,1,0:T(8,128)(2,1)S(1)}, u32[]{:S(2)}, u32[]{:S(2)}) %all-to-all-start.1) | async-done | bytes 458784 | tf_op jit(solution)/shard_map/all_to_all | solution.py:56
  70.8 0.7 gather_fusion
  71.6 0.1 gather.7
  71.7 1.1 %multiply_reduce_fusion = bf16[16,1792]{1,0:T(8,128)(2,1)} fusion(bf16[16,4,1792]{2,1,0:T(4,128)(2,1)S(1)} %gather.7, f32[16,4]{1,0:T(8,128)S(1)} %copy.21, pred[16,4]{1,0:T(8,128)(4,1)S(1)} %get-tuple-element.4), kind=kLoop, calls=%fused_computation.18 | loop fusion | flops 430080 | bytes 287040 | tf_op jit(solution)/shard_map/reduce_sum | solution.py:76
  (21 shorter events, 0.1 us)
Async XLA Ops:
  7.2 36.8 %copy-start = (bf16[4,256,512]{2,1,0:T(8,128)(2,1)S(1)}, bf16[4,256,512]{2,1,0:T(8,128)(2,1)}, u32[]{:S(2)}) copy-start(bf16[4,256,512]{2,1,0:T(8,128)(2,1)} %param.19) | copy-start | bytes 3145732
  7.2 42.4 %reduce-scatter.2.cloned.1.call-start = ((), (), s32[]{:S(2)}) async-start(), calls=%async_computation.3 | async-start | bytes 2752512 | tf_op jit(solution)/shard_map/reduce_scatter | solution.py:52
  35.4 5.9 %copy-start.1 = (bf16[16,1792]{1,0:T(8,128)(2,1)S(1)}, bf16[16,1792]{1,0:T(8,128)(2,1)}, u32[]{:S(2)}) copy-start(bf16[16,1792]{1,0:T(8,128)(2,1)} %param.11) | copy-start | bytes 172036
  35.4 5.9 %copy-start.5 = (bf16[1792,8]{0,1:T(8,128)(2,1)S(1)}, bf16[1792,8]{0,1:T(8,128)(2,1)}, u32[]{:S(2)}) copy-start(bf16[1792,8]{0,1:T(8,128)(2,1)} %param.13) | copy-start | bytes 86020
  35.4 8.4 %copy-start.6 = (s32[16,4]{0,1:T(4,128)S(1)}, s32[16,4]{0,1:T(4,128)}, u32[]{:S(2)}) copy-start(s32[16,4]{0,1:T(4,128)} %param.12) | copy-start | bytes 772
  35.4 8.6 %copy-start.2 = (bf16[4,32,512]{2,1,0:T(8,128)(2,1)S(1)}, bf16[4,32,512]{2,1,0:T(8,128)(2,1)}, u32[]{:S(2)}) copy-start(bf16[4,32,512]{2,1,0:T(8,128)(2,1)} %param.17) | copy-start | bytes 393220
  41.1 16.3 %copy-start.7 = (s32[4]{0:T(128)S(1)}, s32[4]{0:T(128)}, u32[]{:S(2)}) copy-start(s32[4]{0:T(128)} %param.21) | copy-start | bytes 52
  41.1 16.4 %copy-start.3 = (bf16[4,64,256]{2,1,0:T(8,128)(2,1)S(1)}, bf16[4,64,256]{2,1,0:T(8,128)(2,1)}, u32[]{:S(2)}) copy-start(bf16[4,64,256]{2,1,0:T(8,128)(2,1)} %param.20) | copy-start | bytes 393220
  41.1 16.4 %copy-start.4 = (bf16[4,32,64]{2,1,0:T(8,128)(2,1)S(1)}, bf16[4,32,64]{2,1,0:T(8,128)(2,1)}, u32[]{:S(2)}) copy-start(bf16[4,32,64]{2,1,0:T(8,128)(2,1)} %param.18) | copy-start | bytes 49156
  51.6 19.3 %all-to-all-start.1 = ((bf16[8,16,1792]{2,1,0:T(8,128)(2,1)}), bf16[8,16,1792]{2,1,0:T(8,128)(2,1)S(1)}, u32[]{:S(2)}, u32[]{:S(2)}) async-start(bf16[8,16,1792]{2,1,0:T(8,128)(2,1)} %bitcast.5), calls=%async_computation.2 | async-start | bytes 917504 | tf_op jit(solution)/shard_map/all_to_all | solution.py:56
Sparse Core Ops, SparseCore 0:
  41.2 8.2 reduce-scatter.1
where the time goes:
time: 80 us; the launch traced here: 79.6 us
  blocking collectives  25.2 us (32%)
  waiting for transfers between devices  17.2 us (22%)
  between operations  14.2 us (18%)
  matrix products  11.2 us (14%)
  starting transfers between devices  5.91 us (7%)
  other arithmetic  3.88 us (5%)
  local copies, waits for them, and re-layouts  2.09 us (3%)
    all_to_all x1, blocking collectives, local(): lax.all_to_all(outgoing, 'ep', split_axis=0, concat_axis=0, tiled=True)  20.3 us
    all_to_all x1, waiting for transfers between devices, local(): lax.all_to_all(summed, 'ep', split_axis=0, concat_axis=0, tiled=True)  12 us
    all_to_all x1, starting transfers between devices, local(): lax.all_to_all(summed, 'ep', split_axis=0, concat_axis=0, tiled=True)  5.87 us
    dot_general x1, matrix products, local(): jnp.dot(active, down_weight[0], preferred_element_type=jnp.float32)  5.69 us
    reduce_scatter x1, waiting for transfers between devices, local(): lax.psum_scatter(partial_out, 'tp', scatter_dimension=1, tiled=True)  5.18 us
    dot_general x1, matrix products, local(): jnp.dot(flat_rows, gate_weight[0], preferred_element_type=jnp.float32)  2.68 us
    psum x1, blocking collectives, local(): logits = lax.psum(partial_logits, 'tp')  2.46 us
    all_gather x1, blocking collectives, local(): received = lax.all_gather(received, 'tp', axis=2, tiled=True)  2.45 us
  transfers between devices with their start and end apart: 2, of which 2 were waited for; matrix products, arithmetic and copies ran while one was open for 3% of the time, Pallas kernels for 0%

commit v1 on v0

--- a/solution.py
+++ b/solution.py
@@ -1,13 +1,20 @@
+import functools
+
 import jax
 import jax.numpy as jnp
 from jax import lax
+from jax.experimental import pallas as pl
+from jax.experimental.pallas import tpu as pltpu
 from jax.sharding import PartitionSpec as P
+
+MESH = pl.DeviceIdType.MESH
+lanes = 128
 
 softmax_scale = 192.0 ** (-0.5)
 routed_scale = 2.5
 
 
-def local(
+def dispatched(
     hidden,
     routes,
     router_weight,
@@ -77,6 +84,394 @@
     return (moe_out, attn_latent)
 
 
+def fused_kernel(
+    columns,
+    hidden,
+    routes,
+    router_weight,
+    gate_weight,
+    up_weight,
+    down_weight,
+    q_latent,
+    q_rope,
+    cache_latent,
+    cache_rope,
+    lengths,
+    moe_out,
+    attn_out,
+    rows_all,
+    routes_v,
+    router_v,
+    gate_v,
+    up_v,
+    down_v,
+    q_v,
+    qr_v,
+    cl_v,
+    cr_v,
+    logit_v,
+    act_v,
+    tp_out,
+    tp_in,
+    y_out,
+    y_in,
+    keep,
+    z_out,
+    z_in,
+    load_sem,
+    up_send,
+    down_send,
+    cross_send,
+    core_send,
+    line_recv,
+    cross_recv,
+    core_recv,
+    logit_sem,
+    tp_sem,
+    y_sem,
+    z_send,
+    z_recv,
+):
+    tokens, features = hidden.shape
+    experts = rows_all.shape[1] // tokens
+    line = experts // 2
+    chunks = features // columns
+    me = lax.axis_index("ep")
+    core = lax.axis_index("tp")
+    other = 1 - core
+    z = me // 2
+    y = me % 2
+    across = me + 1 - 2 * y
+
+    def rows_of(s, side):
+        return pl.ds(pl.multiple_of((s * 2 + side) * tokens, tokens), tokens)
+
+    local_loads = [
+        (hidden, rows_all.at[core, rows_of(z, y), pl.ds(0, features)]),
+        (routes, routes_v),
+        (q_latent, q_v),
+        (q_rope, qr_v),
+        (cache_latent, cl_v),
+        (cache_rope, cr_v),
+        (router_weight, router_v),
+        (gate_weight.at[0, pl.ds(0, features), :], gate_v.at[0]),
+        (gate_weight.at[0, pl.ds(features, features), :], gate_v.at[1]),
+        (up_weight.at[0, pl.ds(0, features), :], up_v.at[0]),
+        (up_weight.at[0, pl.ds(features, features), :], up_v.at[1]),
+        (down_weight.at[0, :, pl.ds(0, features)], down_v.at[0]),
+        (down_weight.at[0, :, pl.ds(features, features)], down_v.at[1]),
+    ]
+    loads = [
+        pltpu.make_async_copy(src, dst, load_sem.at[i]) for i, (src, dst) in enumerate(local_loads)
+    ]
+    for load in loads:
+        load.start()
+
+    barrier = pltpu.get_barrier_semaphore()
+    pl.semaphore_signal(barrier, inc=1, device_id={"tp": other}, device_id_type=MESH)
+    pl.semaphore_signal(barrier, inc=1, device_id={"ep": across}, device_id_type=MESH)
+    for d in range(1, line):
+        pl.semaphore_signal(
+            barrier, inc=1, device_id={"ep": ((z + d) % line) * 2 + y}, device_id_type=MESH
+        )
+
+    loads[1].wait()
+    expert_lane = lax.broadcasted_iota(jnp.int32, (tokens, lanes), 1)
+    chosen_mask = jnp.zeros((tokens, lanes), jnp.float32)
+    for k in range(routes.shape[1]):
+        chosen_mask += (routes_v[:, k : k + 1] == expert_lane).astype(jnp.float32)
+    rows_all[core, rows_of(z, y), features:] = chosen_mask.astype(jnp.bfloat16)
+    loads[0].wait()
+    pl.semaphore_wait(barrier, line + 1)
+
+    def rows_copy(s, side, send_sem, recv_sem, device):
+        block = rows_all.at[core, rows_of(s, side), :]
+        return pltpu.make_async_remote_copy(
+            src_ref=block,
+            dst_ref=block,
+            send_sem=send_sem,
+            recv_sem=recv_sem,
+            device_id=device,
+            device_id_type=MESH,
+        )
+
+    def to_up(s):
+        return rows_copy(s, y, up_send.at[s], line_recv.at[s], {"ep": me + 2})
+
+    def to_down(s):
+        return rows_copy(s, y, down_send.at[s], line_recv.at[s], {"ep": me - 2})
+
+    def to_across(s):
+        return rows_copy(s, y, cross_send.at[s], cross_recv.at[s], {"ep": across})
+
+    def from_across(s):
+        return rows_copy(s, 1 - y, cross_send.at[s], cross_recv.at[s], {"ep": across})
+
+    def to_core(s, side):
+        index = s * 2 + side
+        return rows_copy(s, side, core_send.at[index], core_recv.at[index], {"tp": other})
+
+    def from_core(index):
+        block = rows_all.at[other, pl.ds(index * tokens, tokens), :]
+        return pltpu.make_async_remote_copy(
+            src_ref=block,
+            dst_ref=block,
+            send_sem=core_send.at[index],
+            recv_sem=core_recv.at[index],
+            device_id={"tp": other},
+            device_id_type=MESH,
+        )
+
+    def attend(b):
+        scores = lax.dot_general(
+            q_v[b], cl_v[b], (((1,), (1,)), ((), ())), preferred_element_type=jnp.float32
+        )
+        scores += jnp.dot(qr_v[b], cr_v[b], preferred_element_type=jnp.float32)
+        scores *= softmax_scale
+        live = lax.broadcasted_iota(jnp.int32, scores.shape, 1) < lengths[b]
+        scores = jnp.where(live, scores, -jnp.inf)
+        highest = jnp.max(scores, axis=1, keepdims=True)
+        expo = jnp.where(live, jnp.exp(scores - highest), 0.0)
+        probs = (expo / jnp.sum(expo, axis=1, keepdims=True)).astype(jnp.bfloat16)
+        mixed = jnp.dot(probs, cl_v[b], preferred_element_type=jnp.float32)
+        attn_out[b] = mixed.astype(attn_out.dtype)
+
+    can_up = z < line - 1
+    can_down = z > 0
+    pl.when(can_up)(lambda: to_up(z).start())
+    pl.when(can_down)(lambda: to_down(z).start())
+    to_across(z).start()
+    to_core(z, y).start()
+
+    for load in loads[2:6]:
+        load.wait()
+    seqs = q_v.shape[0]
+    for r in range(1, line + 1):
+        for b in range(seqs * (r - 1) // line, seqs * r // line):
+            attend(b)
+        if r < line:
+
+            @pl.when(z >= r)
+            def _():
+                s = z - r
+                to_up(s).wait_recv()
+                pl.when(can_up)(lambda: to_up(s).start())
+                to_across(s).start()
+                to_core(s, y).start()
+
+            @pl.when(z + r < line)
+            def _():
+                s = z + r
+                to_down(s).wait_recv()
+                pl.when(can_down)(lambda: to_down(s).start())
+                to_across(s).start()
+                to_core(s, y).start()
+
+        def crossed(s):
+            from_across(s).wait_recv()
+            to_core(s, 1 - y).start()
+
+        if r == 1:
+            crossed(z)
+        else:
+            pl.when(z >= r - 1)(lambda: crossed(z - (r - 1)))
+            pl.when(z + r - 1 < line)(lambda: crossed(z + r - 1))
+
+    loads[6].wait()
+    own = rows_all[core, :, :features]
+    logit_v[0] = jnp.zeros(logit_v.shape[1:], jnp.float32)
+    logit_v[0, :, :experts] = jnp.dot(own, router_v[...], preferred_element_type=jnp.float32)
+    logit_copy = pltpu.make_async_remote_copy(
+        src_ref=logit_v.at[0],
+        dst_ref=logit_v.at[1],
+        send_sem=logit_sem.at[0],
+        recv_sem=logit_sem.at[1],
+        device_id={"tp": other},
+        device_id_type=MESH,
+    )
+    logit_copy.start()
+
+    for load in loads[7:11]:
+        load.wait()
+    gate_part = jnp.dot(own, gate_v[core], preferred_element_type=jnp.float32)
+    up_part = jnp.dot(own, up_v[core], preferred_element_type=jnp.float32)
+    for index in range(experts):
+        from_core(index).wait_recv()
+    theirs = rows_all[other, :, :features]
+    gate_part += jnp.dot(theirs, gate_v[other], preferred_element_type=jnp.float32)
+    up_part += jnp.dot(theirs, up_v[other], preferred_element_type=jnp.float32)
+    act_v[...] = (gate_part / (1.0 + jnp.exp(-gate_part)) * up_part).astype(jnp.bfloat16)
+
+    logit_copy.wait_recv()
+    affinity = 1.0 / (1.0 + jnp.exp(-(logit_v[0] + logit_v[1])))
+    chosen = affinity * rows_all[core, :, features:].astype(jnp.float32)
+    expert_lane = lax.broadcasted_iota(jnp.int32, chosen.shape, 1)
+    mine = jnp.sum(jnp.where(expert_lane == me, chosen, 0.0), axis=1, keepdims=True)
+    gate = routed_scale * mine / jnp.sum(chosen, axis=1, keepdims=True)
+
+    for load in loads[11:]:
+        load.wait()
+
+    def tp_copy(j):
+        return pltpu.make_async_remote_copy(
+            src_ref=tp_out.at[j],
+            dst_ref=tp_in.at[j],
+            send_sem=tp_sem.at[0, j],
+            recv_sem=tp_sem.at[1, j],
+            device_id={"tp": other},
+            device_id_type=MESH,
+        )
+
+    def y_copy(j):
+        return pltpu.make_async_remote_copy(
+            src_ref=y_out.at[j],
+            dst_ref=y_in.at[j],
+            send_sem=y_sem.at[0, j],
+            recv_sem=y_sem.at[1, j],
+            device_id={"ep": across},
+            device_id_type=MESH,
+        )
+
+    def z_copy(j, d):
+        target = (z + d) % line
+        return pltpu.make_async_remote_copy(
+            src_ref=z_out.at[j, target],
+            dst_ref=z_in.at[j, d - 1],
+            send_sem=z_send.at[j, d - 1],
+            recv_sem=z_recv.at[j, d - 1],
+            device_id={"ep": target * 2 + y},
+            device_id_type=MESH,
+        )
+
+    def expert_columns(half, j):
+        part = jnp.dot(
+            act_v[...],
+            down_v[half, :, j * columns : (j + 1) * columns],
+            preferred_element_type=jnp.float32,
+        )
+        return part * gate
+
+    for j in range(chunks):
+        tp_out[j] = expert_columns(other, j).astype(jnp.bfloat16)
+        tp_copy(j).start()
+
+    def along_line(j):
+        y_copy(j).wait_recv()
+        total = keep[j] + y_in[j].astype(jnp.float32)
+        keep[j] = total
+        z_out[j] = total.astype(jnp.bfloat16)
+        for d in range(1, line):
+            z_copy(j, d).start()
+
+    lag = 3
+    for j in range(chunks):
+        part = expert_columns(core, j)
+        tp_copy(j).wait_recv()
+        part = (part + tp_in[j].astype(jnp.float32)).reshape(line, 2, tokens, columns)
+        even, odd = part[:, 0], part[:, 1]
+        y_out[j] = jnp.where(y == 0, odd, even).astype(jnp.bfloat16)
+        y_copy(j).start()
+        keep[j] = jnp.where(y == 0, even, odd)
+        if j >= lag:
+            along_line(j - lag)
+    for j in range(max(chunks - lag, 0), chunks):
+        along_line(j)
+    for j in range(chunks):
+        total = keep[j, z]
+        for d in range(1, line):
+            z_copy(j, d).wait_recv()
+            total += z_in[j, d - 1].astype(jnp.float32)
+        moe_out[:, j * columns : (j + 1) * columns] = total.astype(moe_out.dtype)
+
+    for s in range(line):
+        pl.when(can_up & (s <= z))(lambda: to_up(s).wait_send())
+        pl.when(can_down & (s >= z))(lambda: to_down(s).wait_send())
+        to_across(s).wait_send()
+        to_core(s, 0).wait_send()
+        to_core(s, 1).wait_send()
+    logit_copy.wait_send()
+    for j in range(chunks):
+        tp_copy(j).wait_send()
+        y_copy(j).wait_send()
+        for d in range(1, line):
+            z_copy(j, d).wait_send()
+
+
+def fused(*operands):
+    hidden, routes = operands[:2]
+    tokens, features = hidden.shape
+    experts = lax.axis_size("ep")
+    line = experts // 2
+    hidden_units = operands[3].shape[2]
+    seqs, heads, latent = operands[6].shape
+    rope = operands[7].shape[2]
+    cache = operands[8].shape[1]
+    columns = 256 if features % 256 == 0 else lanes
+    chunks = features // columns
+    every = experts * tokens
+    bf16, f32 = jnp.bfloat16, jnp.float32
+    dma = pltpu.SemaphoreType.DMA
+    anywhere = pl.BlockSpec(memory_space=pl.ANY)
+    vmem = pl.BlockSpec(memory_space=pltpu.VMEM)
+    return pl.pallas_call(
+        functools.partial(fused_kernel, columns),
+        out_shape=(
+            jax.ShapeDtypeStruct((tokens, features), bf16),
+            jax.ShapeDtypeStruct((seqs, heads, latent), bf16),
+        ),
+        in_specs=[anywhere] * 10 + [pl.BlockSpec(memory_space=pltpu.SMEM)],
+        out_specs=(vmem, vmem),
+        scratch_shapes=[
+            pltpu.VMEM((2, every, features + lanes), bf16),
+            pltpu.VMEM(routes.shape, jnp.int32),
+            pltpu.VMEM(operands[2].shape, bf16),
+            pltpu.VMEM((2, features, hidden_units), bf16),
+            pltpu.VMEM((2, features, hidden_units), bf16),
+            pltpu.VMEM((2, hidden_units, features), bf16),
+            pltpu.VMEM((seqs, heads, latent), bf16),
+            pltpu.VMEM((seqs, heads, rope), bf16),
+            pltpu.VMEM((seqs, cache, latent), bf16),
+            pltpu.VMEM((seqs, rope, cache), bf16),
+            pltpu.VMEM((2, every, lanes), f32),
+            pltpu.VMEM((every, hidden_units), bf16),
+            pltpu.VMEM((chunks, every, columns), bf16),
+            pltpu.VMEM((chunks, every, columns), bf16),
+            pltpu.VMEM((chunks, line, tokens, columns), bf16),
+            pltpu.VMEM((chunks, line, tokens, columns), bf16),
+            pltpu.VMEM((chunks, line, tokens, columns), f32),
+            pltpu.VMEM((chunks, line, tokens, columns), bf16),
+            pltpu.VMEM((chunks, line - 1, tokens, columns), bf16),
+            dma((13,)),
+            dma((line,)),
+            dma((line,)),
+            dma((line,)),
+            dma((experts,)),
+            dma((line,)),
+            dma((line,)),
+            dma((experts,)),
+            dma((2,)),
+            dma((2, chunks)),
+            dma((2, chunks)),
+            dma((chunks, line - 1)),
+            dma((chunks, line - 1)),
+        ],
+        compiler_params=pltpu.CompilerParams(
+            collective_id=0, has_side_effects=True, vmem_limit_bytes=60 * 1024 * 1024
+        ),
+    )(*operands)
+
+
+def local(*operands):
+    tokens, top = operands[1].shape
+    experts = lax.axis_size("ep")
+    capacity = min(tokens, 4 * tokens * top // experts)
+    whole_tiles = tokens % 16 == 0 and operands[0].shape[1] % lanes == 0
+    if capacity == tokens and lax.axis_size("tp") == 2 and experts % 2 == 0 and whole_tiles:
+        if 4 <= experts <= 16:
+            return fused(*operands)
+    return dispatched(*operands)
+
+
 def solution(mesh):
     return jax.shard_map(
         local,

time: 80 us -> 42.9 us (0.54)
  Pallas kernels: 0 us -> 35.9 us
  blocking collectives: 25.2 us -> 0 us
  waiting for transfers between devices: 17.2 us -> 0 us
  between operations: 14.2 us -> 0.64 us
  matrix products: 11.2 us -> 0 us
  starting transfers between devices: 5.91 us -> 0 us
  local copies, waits for them, and re-layouts: 2.09 us -> 6.09 us
  other arithmetic: 3.88 us -> 0 us
    pallas_call x0 -> x1, Pallas kernels: none -> 35.9 us  [fused(): pl.pallas_call(functools.partial(fused_kernel, columns), out_shape=(jax.S...]
    all_to_all x1 -> x0, blocking collectives: 20.3 us -> none  [local(): lax.all_to_all(outgoing, 'ep', split_axis=0, concat_axis=0, tiled=True)]
    all_to_all x1 -> x0, waiting for transfers between devices: 12 us -> none  [local(): lax.all_to_all(summed, 'ep', split_axis=0, concat_axis=0, tiled=True)]
    dot_general x7 -> x0, matrix products: 11.2 us -> none  [the longest x1 5.69 us: local(): jnp.dot(active, down_weight[0], preferred_element_type=jnp.float32)]
    all_to_all x1 -> x0, starting transfers between devices: 5.87 us -> none  [local(): lax.all_to_all(summed, 'ep', split_axis=0, concat_axis=0, tiled=True)]
    unnamed x17 -> x4, local copies, waits for them, and re-layouts: 0.88 us -> 6.09 us
    reduce_scatter x1 -> x0, waiting for transfers between devices: 5.18 us -> none  [local(): lax.psum_scatter(partial_out, 'tp', scatter_dimension=1, tiled=True)]
    psum x1 -> x0, blocking collectives: 2.46 us -> none  [local(): logits = lax.psum(partial_logits, 'tp')]
  transfers between devices with their start and end apart: 2 -> 0, of which waited for: 2 -> 0; matrix products, arithmetic and copies ran while one was open for 3% -> 0% of each run, Pallas kernels for 0% -> 0%
where the time goes in v1:
time: 42.9 us; the launch traced here: 42.6 us
  Pallas kernels  35.9 us (84%)
  local copies, waits for them, and re-layouts  6.09 us (14%)
  between operations  0.64 us (1%)
    pallas_call x1, Pallas kernels, fused(): pl.pallas_call(functools.partial(fused_kernel, columns), out_shape=(jax.S...  35.9 us
    unnamed x4, local copies, waits for them, and re-layouts  6.09 us

profile of v1, /device:TPU:0, one launch (start us, length us, event | category | flops | bytes accessed | tf_op | source)
XLA Modules:
  0.0 42.6 jit_solution(114144141583378315)
XLA Ops:
  0.6 1.4 %copy.13.routes = s32[16,4]{1,0:T(8,128)} copy(s32[16,4]{0,1:T(4,128)} %param.12) | data formatting | bytes 512 | tf_op args[1]
  2.0 1.7 %copy.14.router_weight = bf16[1792,8]{1,0:T(8,128)(2,1)} copy(bf16[1792,8]{0,1:T(8,128)(2,1)} %param.13) | data formatting | bytes 57344 | tf_op args[2]
  3.7 35.9 %shard_map.122 = (bf16[16,1792]{1,0:T(8,128)(2,1)}, bf16[4,32,512]{2,1,0:T(8,128)(2,1)}) custom-call(bf16[16,1792]{1,0:T(8,128)(2,1)} %hidden.1, s32[16,4]{1,0:T(8,128)} %copy.13.routes, bf16[1792,8]{1,0:T(8,128)(2,1)} %copy.14.router_weight, bf16[1,3584,512]{2,1,0:T(8,128)(2,1)} %gate_weight.1, bf16[1,3584,512]{2,1,0:T(8,128)(2,1)} %up_weight.1, ...), custom_call_target="tpu_custom_call" | custom-call | tf_op jit(solution)/shard_map/pallas_call | solution.py:416
  39.6 1.4 %copy.17 = bf16[16,1792]{1,0:T(8,128)(2,1)} copy(bf16[16,1792]{1,0:T(8,128)(2,1)} %get-tuple-element.4) | data formatting | bytes 114688
  41.0 1.6 %copy.18 = bf16[4,32,512]{2,1,0:T(8,128)(2,1)} copy(bf16[4,32,512]{2,1,0:T(8,128)(2,1)} %get-tuple-element.5) | data formatting | bytes 262144

commit v2 on v1

--- a/solution.py
+++ b/solution.py
@@ -86,6 +86,7 @@
 
 def fused_kernel(
     columns,
+    parts,
     hidden,
     routes,
     router_weight,
@@ -170,22 +171,41 @@
     barrier = pltpu.get_barrier_semaphore()
     pl.semaphore_signal(barrier, inc=1, device_id={"tp": other}, device_id_type=MESH)
     pl.semaphore_signal(barrier, inc=1, device_id={"ep": across}, device_id_type=MESH)
-    for d in range(1, line):
-        pl.semaphore_signal(
-            barrier, inc=1, device_id={"ep": ((z + d) % line) * 2 + y}, device_id_type=MESH
-        )
+    can_up = z < line - 1
+    can_down = z > 0
+
+    def greet(target):
+        pl.semaphore_signal(barrier, inc=1, device_id={"ep": target}, device_id_type=MESH)
+
+    pl.when(can_up)(lambda: greet(me + 2))
+    pl.when(can_down)(lambda: greet(me - 2))
 
     loads[1].wait()
-    expert_lane = lax.broadcasted_iota(jnp.int32, (tokens, lanes), 1)
+    token_row = lax.broadcasted_iota(jnp.int32, (tokens, lanes), 0)
+    token_lane = lax.broadcasted_iota(jnp.int32, (tokens, lanes), 1)
+    place = (token_lane == token_row + me * tokens).astype(jnp.bfloat16)
+    spread = jnp.dot(
+        routes_v[...].astype(jnp.float32).astype(jnp.bfloat16),
+        place,
+        preferred_element_type=jnp.float32,
+    )
+    expert_row = token_row.astype(jnp.float32)
     chosen_mask = jnp.zeros((tokens, lanes), jnp.float32)
-    for k in range(routes.shape[1]):
-        chosen_mask += (routes_v[:, k : k + 1] == expert_lane).astype(jnp.float32)
+    for k in range(routes.shape[0]):
+        chosen_mask += jnp.where(spread[k : k + 1, :] == expert_row, 1.0, 0.0)
+    inside = (token_lane >= me * tokens) & (token_lane < (me + 1) * tokens)
+    chosen_mask = jnp.where(inside, chosen_mask, 0.0)
     rows_all[core, rows_of(z, y), features:] = chosen_mask.astype(jnp.bfloat16)
     loads[0].wait()
-    pl.semaphore_wait(barrier, line + 1)
-
-    def rows_copy(s, side, send_sem, recv_sem, device):
-        block = rows_all.at[core, rows_of(s, side), :]
+    inner = can_up & can_down
+    pl.when(inner)(lambda: pl.semaphore_wait(barrier, 4))
+    pl.when(jnp.logical_not(inner))(lambda: pl.semaphore_wait(barrier, 3))
+
+    width = rows_all.shape[2] // parts
+
+    def rows_copy(half, index, k, send_sem, recv_sem, device):
+        rows = pl.ds(pl.multiple_of(index * tokens, tokens), tokens)
+        block = rows_all.at[half, rows, pl.ds(k * width, width)]
         return pltpu.make_async_remote_copy(
             src_ref=block,
             dst_ref=block,
@@ -195,32 +215,29 @@
             device_id_type=MESH,
         )
 
-    def to_up(s):
-        return rows_copy(s, y, up_send.at[s], line_recv.at[s], {"ep": me + 2})
-
-    def to_down(s):
-        return rows_copy(s, y, down_send.at[s], line_recv.at[s], {"ep": me - 2})
-
-    def to_across(s):
-        return rows_copy(s, y, cross_send.at[s], cross_recv.at[s], {"ep": across})
-
-    def from_across(s):
-        return rows_copy(s, 1 - y, cross_send.at[s], cross_recv.at[s], {"ep": across})
-
-    def to_core(s, side):
-        index = s * 2 + side
-        return rows_copy(s, side, core_send.at[index], core_recv.at[index], {"tp": other})
-
-    def from_core(index):
-        block = rows_all.at[other, pl.ds(index * tokens, tokens), :]
-        return pltpu.make_async_remote_copy(
-            src_ref=block,
-            dst_ref=block,
-            send_sem=core_send.at[index],
-            recv_sem=core_recv.at[index],
-            device_id={"tp": other},
-            device_id_type=MESH,
-        )
+    def to_up(s, k):
+        sems = up_send.at[s, k], line_recv.at[s, k]
+        return rows_copy(core, s * 2 + y, k, *sems, {"ep": me + 2})
+
+    def to_down(s, k):
+        sems = down_send.at[s, k], line_recv.at[s, k]
+        return rows_copy(core, s * 2 + y, k, *sems, {"ep": me - 2})
+
+    def to_across(s, k):
+        sems = cross_send.at[s, k], cross_recv.at[s, k]
+        return rows_copy(core, s * 2 + y, k, *sems, {"ep": across})
+
+    def from_across(s, k):
+        sems = cross_send.at[s, k], cross_recv.at[s, k]
+        return rows_copy(core, s * 2 + 1 - y, k, *sems, {"ep": across})
+
+    def to_core(index, k):
+        sems = core_send.at[index, k], core_recv.at[index, k]
+        return rows_copy(core, index, k, *sems, {"tp": other})
+
+    def from_core(index, k):
+        sems = core_send.at[index, k], core_recv.at[index, k]
+        return rows_copy(other, index, k, *sems, {"tp": other})
 
     def attend(b):
         scores = lax.dot_general(
@@ -236,51 +253,45 @@
         mixed = jnp.dot(probs, cl_v[b], preferred_element_type=jnp.float32)
         attn_out[b] = mixed.astype(attn_out.dtype)
 
-    can_up = z < line - 1
-    can_down = z > 0
-    pl.when(can_up)(lambda: to_up(z).start())
-    pl.when(can_down)(lambda: to_down(z).start())
-    to_across(z).start()
-    to_core(z, y).start()
+    for k in range(parts):
+        pl.when(can_up)(lambda: to_up(z, k).start())
+        pl.when(can_down)(lambda: to_down(z, k).start())
+        to_across(z, k).start()
+        to_core(me, k).start()
 
     for load in loads[2:6]:
         load.wait()
     seqs = q_v.shape[0]
+    early = seqs // 2
+    for b in range(early):
+        attend(b)
+
+    def forward(s, k, ahead, onward):
+        onward(s, k).wait_recv()
+        pl.when(ahead)(lambda: onward(s, k).start())
+        to_across(s, k).start()
+        to_core(s * 2 + y, k).start()
+
+    def crossed(s, k):
+        from_across(s, k).wait_recv()
+        to_core(s * 2 + 1 - y, k).start()
+
     for r in range(1, line + 1):
-        for b in range(seqs * (r - 1) // line, seqs * r // line):
-            attend(b)
-        if r < line:
-
-            @pl.when(z >= r)
-            def _():
-                s = z - r
-                to_up(s).wait_recv()
-                pl.when(can_up)(lambda: to_up(s).start())
-                to_across(s).start()
-                to_core(s, y).start()
-
-            @pl.when(z + r < line)
-            def _():
-                s = z + r
-                to_down(s).wait_recv()
-                pl.when(can_down)(lambda: to_down(s).start())
-                to_across(s).start()
-                to_core(s, y).start()
-
-        def crossed(s):
-            from_across(s).wait_recv()
-            to_core(s, 1 - y).start()
-
-        if r == 1:
-            crossed(z)
-        else:
-            pl.when(z >= r - 1)(lambda: crossed(z - (r - 1)))
-            pl.when(z + r - 1 < line)(lambda: crossed(z + r - 1))
+        for k in range(parts):
+            if r < line:
+                pl.when(z >= r)(lambda: forward(z - r, k, can_up, to_up))
+                pl.when(z + r < line)(lambda: forward(z + r, k, can_down, to_down))
+            if r == 1:
+                crossed(z, k)
+            else:
+                pl.when(z >= r - 1)(lambda: crossed(z - (r - 1), k))
+                pl.when(z + r - 1 < line)(lambda: crossed(z + r - 1, k))
 
     loads[6].wait()
     own = rows_all[core, :, :features]
-    logit_v[0] = jnp.zeros(logit_v.shape[1:], jnp.float32)
-    logit_v[0, :, :experts] = jnp.dot(own, router_v[...], preferred_element_type=jnp.float32)
+    logit_v[0] = lax.dot_general(
+        router_v[...], own, (((1,), (1,)), ((), ())), preferred_element_type=jnp.float32
+    )
     logit_copy = pltpu.make_async_remote_copy(
         src_ref=logit_v.at[0],
         dst_ref=logit_v.at[1],
@@ -296,7 +307,8 @@
     gate_part = jnp.dot(own, gate_v[core], preferred_element_type=jnp.float32)
     up_part = jnp.dot(own, up_v[core], preferred_element_type=jnp.float32)
     for index in range(experts):
-        from_core(index).wait_recv()
+        for k in range(parts):
+            from_core(index, k).wait_recv()
     theirs = rows_all[other, :, :features]
     gate_part += jnp.dot(theirs, gate_v[other], preferred_element_type=jnp.float32)
     up_part += jnp.dot(theirs, up_v[other], preferred_element_type=jnp.float32)
@@ -304,10 +316,12 @@
 
     logit_copy.wait_recv()
     affinity = 1.0 / (1.0 + jnp.exp(-(logit_v[0] + logit_v[1])))
-    chosen = affinity * rows_all[core, :, features:].astype(jnp.float32)
-    expert_lane = lax.broadcasted_iota(jnp.int32, chosen.shape, 1)
-    mine = jnp.sum(jnp.where(expert_lane == me, chosen, 0.0), axis=1, keepdims=True)
-    gate = routed_scale * mine / jnp.sum(chosen, axis=1, keepdims=True)
+    masks = rows_all[core, :, features:].astype(jnp.float32).reshape(experts, tokens, lanes)
+    chosen = affinity * jnp.sum(masks, axis=0)[:experts]
+    expert_row = lax.broadcasted_iota(jnp.int32, chosen.shape, 0)
+    mine = jnp.sum(jnp.where(expert_row == me, chosen, 0.0), axis=0, keepdims=True)
+    gate_row = routed_scale * mine / jnp.sum(chosen, axis=0, keepdims=True)
+    gate = jnp.transpose(jnp.broadcast_to(gate_row, (lanes, lanes)))[:, :1]
 
     for load in loads[11:]:
         load.wait()
@@ -363,7 +377,7 @@
         for d in range(1, line):
             z_copy(j, d).start()
 
-    lag = 3
+    lag = chunks
     for j in range(chunks):
         part = expert_columns(core, j)
         tp_copy(j).wait_recv()
@@ -376,6 +390,8 @@
             along_line(j - lag)
     for j in range(max(chunks - lag, 0), chunks):
         along_line(j)
+    for b in range(early, seqs):
+        attend(b)
     for j in range(chunks):
         total = keep[j, z]
         for d in range(1, line):
@@ -384,11 +400,12 @@
         moe_out[:, j * columns : (j + 1) * columns] = total.astype(moe_out.dtype)
 
     for s in range(line):
-        pl.when(can_up & (s <= z))(lambda: to_up(s).wait_send())
-        pl.when(can_down & (s >= z))(lambda: to_down(s).wait_send())
-        to_across(s).wait_send()
-        to_core(s, 0).wait_send()
-        to_core(s, 1).wait_send()
+        for k in range(parts):
+            pl.when(can_up & (s <= z))(lambda: to_up(s, k).wait_send())
+            pl.when(can_down & (s >= z))(lambda: to_down(s, k).wait_send())
+            to_across(s, k).wait_send()
+            to_core(s * 2, k).wait_send()
+            to_core(s * 2 + 1, k).wait_send()
     logit_copy.wait_send()
     for j in range(chunks):
         tp_copy(j).wait_send()
@@ -397,8 +414,9 @@
             z_copy(j, d).wait_send()
 
 
-def fused(*operands):
-    hidden, routes = operands[:2]
+def fused(hidden, routes, router_weight, *others):
+    operands = (hidden, routes.T, router_weight.T) + others
+    routes = operands[1]
     tokens, features = hidden.shape
     experts = lax.axis_size("ep")
     line = experts // 2
@@ -408,18 +426,19 @@
     cache = operands[8].shape[1]
     columns = 256 if features % 256 == 0 else lanes
     chunks = features // columns
+    parts = 3 if (features // lanes + 1) % 3 == 0 else 1
     every = experts * tokens
     bf16, f32 = jnp.bfloat16, jnp.float32
     dma = pltpu.SemaphoreType.DMA
-    anywhere = pl.BlockSpec(memory_space=pl.ANY)
+    in_hbm = pl.BlockSpec(memory_space=pltpu.HBM)
     vmem = pl.BlockSpec(memory_space=pltpu.VMEM)
     return pl.pallas_call(
-        functools.partial(fused_kernel, columns),
+        functools.partial(fused_kernel, columns, parts),
         out_shape=(
             jax.ShapeDtypeStruct((tokens, features), bf16),
             jax.ShapeDtypeStruct((seqs, heads, latent), bf16),
         ),
-        in_specs=[anywhere] * 10 + [pl.BlockSpec(memory_space=pltpu.SMEM)],
+        in_specs=[in_hbm] * 10 + [pl.BlockSpec(memory_space=pltpu.SMEM)],
         out_specs=(vmem, vmem),
         scratch_shapes=[
             pltpu.VMEM((2, every, features + lanes), bf16),
@@ -432,7 +451,7 @@
             pltpu.VMEM((seqs, heads, rope), bf16),
             pltpu.VMEM((seqs, cache, latent), bf16),
             pltpu.VMEM((seqs, rope, cache), bf16),
-            pltpu.VMEM((2, every, lanes), f32),
+            pltpu.VMEM((2, experts, lanes), f32),
             pltpu.VMEM((every, hidden_units), bf16),
             pltpu.VMEM((chunks, every, columns), bf16),
             pltpu.VMEM((chunks, every, columns), bf16),
@@ -442,13 +461,13 @@
             pltpu.VMEM((chunks, line, tokens, columns), bf16),
             pltpu.VMEM((chunks, line - 1, tokens, columns), bf16),
             dma((13,)),
-            dma((line,)),
-            dma((line,)),
-            dma((line,)),
-            dma((experts,)),
-            dma((line,)),
-            dma((line,)),
-            dma((experts,)),
+            dma((line, parts)),
+            dma((line, parts)),
+            dma((line, parts)),
+            dma((experts, parts)),
+            dma((line, parts)),
+            dma((line, parts)),
+            dma((experts, parts)),
             dma((2,)),
             dma((2, chunks)),
             dma((2, chunks)),
@@ -467,7 +486,7 @@
     capacity = min(tokens, 4 * tokens * top // experts)
     whole_tiles = tokens % 16 == 0 and operands[0].shape[1] % lanes == 0
     if capacity == tokens and lax.axis_size("tp") == 2 and experts % 2 == 0 and whole_tiles:
-        if 4 <= experts <= 16:
+        if experts in (4, 8) and experts * tokens == lanes:
             return fused(*operands)
     return dispatched(*operands)
 

time: 42.9 us -> 37.9 us (0.88)
  local copies, waits for them, and re-layouts: 6.09 us -> 3.01 us
  Pallas kernels: 35.9 us -> 34.1 us
    unnamed x4 -> x2, local copies, waits for them, and re-layouts: 6.09 us -> 3.01 us
    pallas_call x1, Pallas kernels: 35.9 us -> 34.1 us  [fused(): pl.pallas_call(functools.partial(fused_kernel, columns, parts), out_shape...]
where the time goes in v2:
time: 37.9 us; the launch traced here: 37.7 us
  Pallas kernels  34.1 us (90%)
  local copies, waits for them, and re-layouts  3.01 us (8%)
  between operations  0.64 us (2%)
    pallas_call x1, Pallas kernels, fused(): pl.pallas_call(functools.partial(fused_kernel, columns, parts), out_shape...  34.1 us
    unnamed x2, local copies, waits for them, and re-layouts  3.01 us

profile of v2, /device:TPU:0, one launch (start us, length us, event | category | flops | bytes accessed | tf_op | source)
XLA Modules:
  0.0 37.7 jit_solution(10438143492241065552)
XLA Ops:
  0.6 34.1 %shard_map.122 = (bf16[16,1792]{1,0:T(8,128)(2,1)}, bf16[4,32,512]{2,1,0:T(8,128)(2,1)}) custom-call(bf16[16,1792]{1,0:T(8,128)(2,1)} %hidden.1, s32[4,16]{1,0:T(4,128)} %bitcast.3, bf16[8,1792]{1,0:T(8,128)(2,1)} %bitcast.2, bf16[1,3584,512]{2,1,0:T(8,128)(2,1)} %gate_weight.1, bf16[1,3584,512]{2,1,0:T(8,128)(2,1)} %up_weight.1, ...), custom_call_target="tpu_custom_call" | custom-call | tf_op jit(solution)/shard_map/pallas_call | solution.py:435
  34.7 1.4 %copy.15 = bf16[16,1792]{1,0:T(8,128)(2,1)} copy(bf16[16,1792]{1,0:T(8,128)(2,1)} %get-tuple-element.4) | data formatting | bytes 114688
  36.1 1.6 %copy.16 = bf16[4,32,512]{2,1,0:T(8,128)(2,1)} copy(bf16[4,32,512]{2,1,0:T(8,128)(2,1)} %get-tuple-element.5) | data formatting | bytes 262144
